TPU v7x, 32 devices: a whole 2x2x4 slice. The times are simulated.
32 devices in a mesh: pool: 4 (over x, core), rp: 8 (over z, y).
Axes of the slice: x: 2, y: 2, z: 4, core: 2. Of those that a mesh axis runs over, the one named last changes fastest.
Arguments:
- wannier_coupling: bfloat16 [2, 512, 5184], P(None, ('pool', 'rp')), may hold values from -0.25 to 0.25
- lattice_vectors: int32 [3, 512], P(None, ('pool', 'rp')), may hold values from -12 to 12
- degeneracy: int32 [1, 512], P(None, ('pool', 'rp')), may hold values from 1 to 4
- fine_points: int32 [3, 32], P(None, 'pool'), may hold values from 0 to 47
- mode_vectors: float32 [32, 2, 9, 9], P('pool'), may hold values from -2 to 2
- bands_shifted: float32 [32, 2, 24, 24], P(('pool', 'rp')), may hold values from -1.25 to 1.25
- bands_anchor: float32 [2, 24, 24], replicated, may hold values from -1.25 to 1.25
Outputs:
- coupling: float32 [32, 2, 9, 576], P(('pool', 'rp'))
All inputs are finite; a program needn't handle non-finite values.
Results may differ from a plain program's by a relative error of at most 0.0021.
Values may be sent and summed in bfloat16 or wider, within the bound.
A program may use at most 64 MiB of HBM per device.

v0:
```python
import math

import jax
import jax.numpy as jnp
from jax import lax
from jax.sharding import PartitionSpec as P

NQG = 48


full_turn = 2.0 * math.pi
highest = lax.Precision.HIGHEST


def phase_pair(fine_points, lattice_vectors, degeneracy):
    winding = fine_points[0][:, None] * lattice_vectors[0][None, :]
    winding = winding + fine_points[1][:, None] * lattice_vectors[1][None, :]
    winding = winding + fine_points[2][:, None] * lattice_vectors[2][None, :]
    winding = jnp.mod(winding, NQG)
    angles = winding.astype(jnp.float32) * (full_turn / NQG)
    weights = 1.0 / degeneracy[0].astype(jnp.float32)
    phase_real = (jnp.cos(angles) * weights[None, :]).astype(jnp.bfloat16)
    phase_imag = (jnp.sin(angles) * weights[None, :]).astype(jnp.bfloat16)
    return (phase_real, phase_imag)


def contract_modes(source, matrix):
    return jnp.einsum("qap,qav->qvp", source, matrix, precision=highest)


def rotate_modes(real_part, imag_part, vectors):
    vector_real = vectors[:, 0]
    vector_imag = vectors[:, 1]
    out_real = contract_modes(real_part, vector_real) - contract_modes(imag_part, vector_imag)
    out_imag = contract_modes(real_part, vector_imag) + contract_modes(imag_part, vector_real)
    return (out_real, out_imag)


def rotate_bands(real_part, imag_part, shifted, anchor):
    points = real_part.shape[0]
    mode_count = real_part.shape[1]
    band_count = anchor.shape[1]
    grid_real = real_part.reshape(points, mode_count, band_count, band_count)
    grid_imag = imag_part.reshape(points, mode_count, band_count, band_count)

    def right_product(source, matrix):
        return jnp.einsum("qvmn,nl->qvml", source, matrix, precision=highest)

    def left_product(matrix, source):
        return jnp.einsum("qma,qvml->qval", matrix, source, precision=highest)

    right_real = right_product(grid_real, anchor[0]) - right_product(grid_imag, anchor[1])
    right_imag = right_product(grid_real, anchor[1]) + right_product(grid_imag, anchor[0])
    shift_real = shifted[:, 0]
    shift_imag = shifted[:, 1]
    final_real = left_product(shift_real, right_real) + left_product(shift_imag, right_imag)
    final_imag = left_product(shift_real, right_imag) - left_product(shift_imag, right_real)
    final_real = final_real.reshape(points, mode_count, band_count * band_count)
    final_imag = final_imag.reshape(points, mode_count, band_count * band_count)
    return jnp.stack([final_real, final_imag], axis=1)


def fold_groups(coupling_block, vectors_block, weights_block, fine_points):
    coupling_rows = lax.all_gather(coupling_block, "pool", axis=1, tiled=True)
    vectors_here = lax.all_gather(vectors_block, "pool", axis=1, tiled=True)
    degeneracy_here = lax.all_gather(weights_block, "pool", axis=1, tiled=True)
    phase_real, phase_imag = phase_pair(fine_points, vectors_here, degeneracy_here)
    real_sum = jnp.dot(phase_real, coupling_rows[0], preferred_element_type=jnp.float32) - jnp.dot(
        phase_imag, coupling_rows[1], preferred_element_type=jnp.float32
    )
    imag_sum = jnp.dot(phase_real, coupling_rows[1], preferred_element_type=jnp.float32) + jnp.dot(
        phase_imag, coupling_rows[0], preferred_element_type=jnp.float32
    )
    return (real_sum, imag_sum)


def finish_owner(part_real, part_imag, mode_vectors, bands_shifted, bands_anchor):
    mode_real, mode_imag = rotate_modes(part_real, part_imag, mode_vectors)
    return rotate_bands(
        lax.all_to_all(mode_real, "rp", split_axis=0, concat_axis=2, tiled=True),
        lax.all_to_all(mode_imag, "rp", split_axis=0, concat_axis=2, tiled=True),
        bands_shifted,
        bands_anchor,
    )


def per_device(
    wannier_coupling,
    lattice_vectors,
    degeneracy,
    fine_points,
    mode_vectors,
    bands_shifted,
    bands_anchor,
):
    points = fine_points.shape[1]
    mode_count = mode_vectors.shape[2]
    pair_count = bands_anchor.shape[1] * bands_anchor.shape[2]
    rows_here = wannier_coupling.shape[1]
    shaped = wannier_coupling.reshape(2, rows_here, mode_count, pair_count)
    moved = lax.all_to_all(shaped, "rp", split_axis=3, concat_axis=1, tiled=True)
    group_rows = moved.shape[1]
    moved = moved.reshape(2, group_rows, -1)
    vectors_group, weights_group = (
        lax.all_gather(lattice_vectors, "rp", axis=1, tiled=True),
        lax.all_gather(degeneracy, "rp", axis=1, tiled=True),
    )
    sum_real, sum_imag = fold_groups(moved, vectors_group, weights_group, fine_points)
    part_real = sum_real.reshape(points, mode_count, -1)
    part_imag = sum_imag.reshape(points, mode_count, -1)
    return finish_owner(part_real, part_imag, mode_vectors, bands_shifted, bands_anchor)


def solution(mesh):
    return jax.shard_map(
        per_device,
        mesh=mesh,
        in_specs=(
            P(None, ("pool", "rp"), None),
            P(None, ("pool", "rp")),
            P(None, ("pool", "rp")),
            P(None, "pool"),
            P("pool", None, None, None),
            P(("pool", "rp"), None, None, None),
            P(),
        ),
        out_specs=P(("pool", "rp"), None, None, None),
        check_vma=False,
    )
```

profile of v0, /device:TPU:0, one launch (start us, length us, event | category | flops | bytes accessed | tf_op | source)
XLA Modules:
  0.0 130.1 jit_solution(11146342148523568554)
XLA Ops:
  6.5 1.3 %reshape.64 = bf16[2,16,9,576]{3,2,1,0:T(8,128)(2,1)S(1)} reshape(bf16[2,16,5184]{2,1,0:T(8,128)(2,1)} %param.7) | data formatting | bytes 663552 | tf_op jit(solution)/shard_map/reshape | solution.py:100
  7.9 8.5 %copy.44 = bf16[2,16,9,576]{1,0,2,3:T(2,128)(2,1)S(1)} copy(bf16[2,16,9,576]{3,2,1,0:T(8,128)(2,1)S(1)} %reshape.64) | data formatting | bytes 663552 | tf_op jit(solution)/shard_map/reshape | solution.py:100
  16.4 2.7 %reshape.83 = bf16[8,2,10368]{2,1,0:T(2,128)(2,1)S(1)} reshape(bf16[576,9,2,16]{3,2,1,0:T(2,128)(2,1)S(1)} %bitcast.111) | data formatting | bytes 663552
  19.1 18.1 %all_to_all.45 = bf16[8,2,10368]{2,1,0:T(2,128)(2,1)S(1)} all-to-all(bf16[8,2,10368]{2,1,0:T(2,128)(2,1)S(1)} %reshape.83), channel_id=1, replica_groups=mesh['pool'=4,'rp'=8] {'rp'}, dimensions={0} | all-to-all | bytes 663552 | tf_op jit(solution)/shard_map/all_to_all | solution.py:101
  37.2 1.9 %reshape.84 = bf16[576,9,2,16]{3,2,1,0:T(2,128)(2,1)S(1)} reshape(bf16[8,2,10368]{2,1,0:T(2,128)(2,1)S(1)} %all_to_all.45) | data formatting | bytes 663552
  39.1 4.1 %copy.63 = bf16[2,16,9,8,72]{4,2,1,3,0:T(8,128)(2,1)} copy(bf16[2,16,9,8,72]{1,0,2,4,3:T(2,128)(2,1)S(1)} %bitcast.112) | data formatting | bytes 663552 | tf_op jit(solution)/shard_map/all_to_all | solution.py:101
  43.2 2.6 %reshape.65 = bf16[2,128,648]{2,1,0:T(8,128)(2,1)} reshape(bf16[2,8,16,9,72]{4,3,2,1,0:T(8,128)(2,1)} %bitcast.113) | data formatting | bytes 663552 | tf_op jit(solution)/shard_map/reshape | solution.py:103
  45.9 26.1 %all-gather = s32[8,16,3]{1,2,0:T(4,128)S(1)} all-gather(s32[1,16,3]{1,2,0:T(4,128)S(1)} %bitcast.117), channel_id=1, replica_groups=mesh['pool'=4,'rp'=8] {'rp'}, dimensions={0}, use_global_device_ids=true | all-gather | bytes 1728 | tf_op jit(solution)/shard_map/all_gather | solution.py:105
  72.4 0.6 dynamic-slice
  73.8 7.7 %all-reduce = s32[128]{0:T(128)S(1)} all-reduce(s32[128]{0:T(128)S(1)} %bitcast_dynamic-update-slice_fusion), channel_id=1, replica_groups=mesh['pool'=4,'rp'=8] {'rp'}, use_global_device_ids=true, to_apply=%add | all-reduce | flops 128 | bytes 1024
  81.5 5.0 %all_gather.18 = s32[1,512]{1,0:T(1,128)S(1)} all-gather(s32[1,128]{1,0:T(1,128)S(1)} %bitcast.134), channel_id=1, replica_groups=mesh['pool'=4,'rp'=8] {'pool'}, dimensions={1}, use_global_device_ids=true | all-gather | bytes 2560 | tf_op jit(solution)/shard_map/all_gather | solution.py:66
  86.5 5.2 %all_gather.16 = s32[3,512]{1,0:T(4,128)S(1)} all-gather(s32[3,128]{1,0:T(4,128)S(1)} %bitcast.116), channel_id=1, replica_groups=mesh['pool'=4,'rp'=8] {'pool'}, dimensions={1}, use_global_device_ids=true | all-gather | bytes 7680 | tf_op jit(solution)/shard_map/all_gather | solution.py:65
  91.7 1.6 %fusion.4 = f32[8,648]{1,0:T(8,128)S(1)} fusion(bf16[2,512,648]{2,1,0:T(8,128)(2,1)} %all-gather.3.cloned.1.call-done, f32[512]{0:T(512)S(1)} %bitcast.118, s32[512]{0:T(512)S(1)} %bitcast.126, s32[8]{0:T(128)S(1)} %get-tuple-element.11, s32[512]{0:T(512)S(1)} %bitcast.130, s32[8]{0:T(128)S(1)} %get-tuple-element.12, s32[512]{0:T(512)S(1)} %bitcast.122, ...), kind=kOutput, calls=%fused_computation.14 | convolution fusion | flops 5369856 | bytes 815456 | tf_op jit(solution)/shard_map/dot_general | solution.py:68
  93.3 1.5 %convolution_subtract_fusion.3 = f32[8,648]{1,0:T(8,128)S(1)} fusion(f32[8,648]{1,0:T(8,128)S(1)} %fusion.4, bf16[2,512,648]{2,1,0:T(8,128)(2,1)} %all-gather.3.cloned.1.call-done, f32[512]{0:T(512)S(1)} %bitcast.119, s32[512]{0:T(512)S(1)} %bitcast.127, s32[8]{0:T(128)S(1)} %get-tuple-element.11, s32[512]{0:T(512)S(1)} %bitcast.131, ...), kind=kOutput, calls=%fused_computation.11 | convolution fusion | flops 5375040 | bytes 836192 | tf_op jit(solution)/shard_map/dot_general | solution.py:68
  96.3 0.7 reshape.85
  97.0 5.4 %all-to-all-start.1 = ((f32[8,1,648]{2,1,0:T(1,128)}), f32[8,1,648]{2,1,0:T(1,128)S(1)}, u32[]{:S(2)}, u32[]{:S(2)}) async-start(f32[8,1,648]{2,1,0:T(1,128)} %reshape.85), calls=%async_computation.1 | async-start | bytes 49152 | tf_op jit(solution)/shard_map/all_to_all | solution.py:80
  102.7 0.7 reshape.87
  103.4 5.7 %all-to-all-done.1 = f32[8,1,648]{2,1,0:T(1,128)S(1)} async-done(((f32[8,1,648]{2,1,0:T(1,128)}), f32[8,1,648]{2,1,0:T(1,128)S(1)}, u32[]{:S(2)}, u32[]{:S(2)}) %all-to-all-start.1) | async-done | bytes 20768 | tf_op jit(solution)/shard_map/all_to_all | solution.py:80
  109.1 3.3 %all-to-all-start.2 = ((f32[8,1,648]{2,1,0:T(1,128)}), f32[8,1,648]{2,1,0:T(1,128)S(1)}, u32[]{:S(2)}, u32[]{:S(2)}) async-start(f32[8,1,648]{2,1,0:T(1,128)} %reshape.87), calls=%async_computation.2 | async-start | bytes 49152 | tf_op jit(solution)/shard_map/all_to_all | solution.py:81
  112.4 0.5 broadcast.4
  112.9 0.7 reduce
  114.5 4.5 %all-to-all-done.2 = f32[8,1,648]{2,1,0:T(1,128)S(1)} async-done(((f32[8,1,648]{2,1,0:T(1,128)}), f32[8,1,648]{2,1,0:T(1,128)S(1)}, u32[]{:S(2)}, u32[]{:S(2)}) %all-to-all-start.2) | async-done | bytes 20768 | tf_op jit(solution)/shard_map/all_to_all | solution.py:81
  119.0 0.7 reduce.1
  122.6 0.6 copy.57
  (56 shorter events, 5.9 us)
Async XLA Ops:
  6.5 85.2 %all-gather.3.cloned.1.call-start = ((), (), s32[]{:S(2)}) async-start(), calls=%async_computation.3 | async-start | bytes 1966080 | tf_op jit(solution)/shard_map/all_gather | solution.py:64
  43.2 2.7 %copy-start.3 = (s32[3,16]{1,0:T(4,128)S(1)}, s32[3,16]{1,0:T(4,128)}, u32[]{:S(2)}) copy-start(s32[3,16]{1,0:T(4,128)} %param.8) | copy-start | bytes 580
  43.2 28.9 %copy-start.2 = (f32[8,2,9,9]{3,1,2,0:T(2,128)S(1)}, f32[8,2,9,9]{3,1,2,0:T(2,128)}, u32[]{:S(2)}) copy-start(f32[8,2,9,9]{3,1,2,0:T(2,128)} %param.11) | copy-start | bytes 15556
  43.2 29.2 %copy-start.7 = (u32[32]{0:T(128)S(1)}, u32[32]{0:T(128)}, u32[]{:S(2)}) copy-start(u32[32]{0:T(128)} %constant.22) | copy-start | bytes 388
  43.2 30.5 %copy-start.6 = (s32[1,16]{1,0:T(1,128)S(1)}, s32[1,16]{1,0:T(1,128)}, u32[]{:S(2)}) copy-start(s32[1,16]{1,0:T(1,128)} %param.9) | copy-start | bytes 196
  43.2 48.5 %copy-start.4 = (s32[3,8]{1,0:T(4,128)S(1)}, s32[3,8]{1,0:T(4,128)}, u32[]{:S(2)}) copy-start(s32[3,8]{1,0:T(4,128)} %param.10) | copy-start | bytes 292
  91.7 3.2 %copy-start.5 = (bf16[2,512,648]{2,1,0:T(8,128)(2,1)S(1)}, bf16[2,512,648]{2,1,0:T(8,128)(2,1)}, u32[]{:S(2)}) copy-start(bf16[2,512,648]{2,1,0:T(8,128)(2,1)} %all-gather.3.cloned.1.call-done) | copy-start | bytes 3981316
  94.9 19.0 %copy-start = (f32[2,24,24]{2,1,0:T(8,128)S(1)}, f32[2,24,24]{2,1,0:T(8,128)}, u32[]{:S(2)}) copy-start(f32[2,24,24]{2,1,0:T(8,128)} %param.13) | copy-start | bytes 13828
  95.7 24.9 %copy-start.1 = (f32[1,2,24,24]{3,2,1,0:T(8,128)S(1)}, f32[1,2,24,24]{3,2,1,0:T(8,128)}, u32[]{:S(2)}) copy-start(f32[1,2,24,24]{3,2,1,0:T(8,128)} %param.12) | copy-start | bytes 13828
  97.0 12.1 %all-to-all-start.1 = ((f32[8,1,648]{2,1,0:T(1,128)}), f32[8,1,648]{2,1,0:T(1,128)S(1)}, u32[]{:S(2)}, u32[]{:S(2)}) async-start(f32[8,1,648]{2,1,0:T(1,128)} %reshape.85), calls=%async_computation.1 | async-start | bytes 49152 | tf_op jit(solution)/shard_map/all_to_all | solution.py:80
  109.1 9.9 %all-to-all-start.2 = ((f32[8,1,648]{2,1,0:T(1,128)}), f32[8,1,648]{2,1,0:T(1,128)S(1)}, u32[]{:S(2)}, u32[]{:S(2)}) async-start(f32[8,1,648]{2,1,0:T(1,128)} %reshape.87), calls=%async_computation.2 | async-start | bytes 49152 | tf_op jit(solution)/shard_map/all_to_all | solution.py:81
Sparse Core Ops, SparseCore 0:
  46.0 18.0 all-gather.2
where the time goes:
time: 131 us; the launch traced here: 130 us
  blocking collectives  62.1 us (47%)
  local copies, waits for them, and re-layouts  25.9 us (20%)
  between operations  14.4 us (11%)
  waiting for transfers between devices  10.2 us (8%)
  starting transfers between devices  8.75 us (7%)
  matrix products  7.26 us (6%)
  other arithmetic  1.46 us (1%)
    all_gather x1, blocking collectives, per_device(): lax.all_gather(lattice_vectors, 'rp', axis=1, tiled=True)  26.1 us
    all_to_all x1, blocking collectives, per_device(): lax.all_to_all(shaped, 'rp', split_axis=3, concat_axis=1, tiled=True)  18.1 us
    reshape x2, local copies, waits for them, and re-layouts, per_device(): shaped = wannier_coupling.reshape(2, rows_here, mode_count, pair_count)  9.81 us
    unnamed x1, blocking collectives  7.67 us
    unnamed x28, local copies, waits for them, and re-layouts  7.31 us
    all_to_all x1, waiting for transfers between devices, finish_owner(): lax.all_to_all(mode_real, 'rp', split_axis=0, concat_axis=2, tiled=True)  5.72 us
    all_to_all x1, starting transfers between devices, finish_owner(): lax.all_to_all(mode_real, 'rp', split_axis=0, concat_axis=2, tiled=True)  5.44 us
    all_gather x1, blocking collectives, fold_groups(): vectors_here = lax.all_gather(vectors_block, 'pool', axis=1, tiled=True)  5.18 us
  transfers between devices with their start and end apart: 3, of which 2 were waited for; matrix products, arithmetic and copies ran while one was open for 3% of the time, Pallas kernels for 0%

commit v1 on v0

v1 whole, which is shorter than its diff:
```python
import functools
import math

import jax
import jax.numpy as jnp
from jax import lax
from jax.experimental import pallas as pl
from jax.experimental.pallas import tpu as pltpu
from jax.sharding import PartitionSpec as P

NQG = 48
LANES = 128
SPAN = 1024
WIRE = jnp.float32

full_turn = 2.0 * math.pi
highest = lax.Precision.HIGHEST
MESH = pl.DeviceIdType.MESH


def split_wide(value):
    high = value.astype(jnp.bfloat16)
    low = (value - high.astype(jnp.float32)).astype(jnp.bfloat16)
    return high, low


def build_pairs(shifted_ref, anchor_ref, kron):
    bands = anchor_ref.shape[1]
    pairs = bands * bands
    row = lax.broadcasted_iota(jnp.int32, (bands, pairs), 0).astype(jnp.float32)
    col = lax.broadcasted_iota(jnp.int32, (bands, pairs), 1).astype(jnp.float32)
    outer = jnp.floor((col + 0.5) * (1.0 / bands))
    inner = col - outer * bands
    pick_outer = jnp.where(row == outer, 1.0, 0.0)
    pick_inner = jnp.where(row == inner, 1.0, 0.0)

    def spread(matrix, pick):
        return jnp.dot(matrix, pick, precision=highest, preferred_element_type=jnp.float32)

    shift_real = spread(shifted_ref[0, 0], pick_outer)
    shift_imag = spread(shifted_ref[0, 1], pick_outer)
    anchor_real = spread(anchor_ref[0], pick_inner)
    anchor_imag = spread(anchor_ref[1], pick_inner)
    for start in range(0, bands, 2):
        reals, imags = [], []
        for m in (start, start + 1):
            sr = shift_real[m : m + 1]
            si = shift_imag[m : m + 1]
            reals.append(sr * anchor_real + si * anchor_imag)
            imags.append(sr * anchor_imag - si * anchor_real)
        rows = pl.ds(start * bands, 2 * bands)
        kron[0, rows, :], kron[1, rows, :] = split_wide(jnp.concatenate(reals, axis=0))
        kron[2, rows, :], kron[3, rows, :] = split_wide(jnp.concatenate(imags, axis=0))


def kernel(
    pool,
    rp,
    coupling_ref,
    lattice_ref,
    points_ref,
    modes_ref,
    shifted_ref,
    anchor_ref,
    out_ref,
    rows_all,
    lattice_pair,
    points_all,
    partial,
    wire,
    recv,
    flat,
    kron,
    local_sem,
    pair_send,
    pair_recv,
    small_send,
    small_recv,
    point_send,
    point_recv,
    send_sem,
    recv_sem,
):
    sides = pool // 2
    my_pool = lax.axis_index("pool")
    my_rp = lax.axis_index("rp")
    core = lax.rem(my_pool, 2)
    side = my_pool // 2
    partner = side * 2 + 1 - core
    total = sides * rp
    me = side * rp + my_rp
    points = points_ref.shape[0]

    barrier = pltpu.get_barrier_semaphore()
    pl.semaphore_signal(barrier, inc=1, device_id={"pool": partner, "rp": my_rp}, device_id_type=MESH)

    def target(step):
        other = lax.rem(me + step, total)
        return other, {"pool": (other // rp) * 2 + core, "rp": lax.rem(other, rp)}

    for step in range(1, total):
        pl.semaphore_signal(barrier, inc=1, device_id=target(step)[1], device_id_type=MESH)

    load = pltpu.make_async_copy(coupling_ref, rows_all.at[0], local_sem)
    load.start()
    here = pl.ds(pl.multiple_of(side * points, points), points)
    points_all[here, :] = points_ref[...]

    pl.semaphore_wait(barrier, total)

    pair_id = {"pool": partner, "rp": my_rp}
    small_copy = pltpu.make_async_remote_copy(
        src_ref=lattice_ref, dst_ref=lattice_pair, send_sem=small_send, recv_sem=small_recv,
        device_id=pair_id, device_id_type=MESH)
    small_copy.start()
    point_copies = []
    for step in range(1, sides):
        other_side = lax.rem(side + step, sides)
        copy = pltpu.make_async_remote_copy(
            src_ref=points_ref, dst_ref=points_all.at[here, :],
            send_sem=point_send.at[step - 1], recv_sem=point_recv.at[step - 1],
            device_id={"pool": other_side * 2 + core, "rp": my_rp}, device_id_type=MESH)
        copy.start()
        point_copies.append(copy)
    pair_copy = pltpu.make_async_remote_copy(
        src_ref=coupling_ref, dst_ref=rows_all.at[1], send_sem=pair_send, recv_sem=pair_recv,
        device_id=pair_id, device_id_type=MESH)
    pair_copy.start()

    build_pairs(shifted_ref, anchor_ref, kron)

    small_copy.wait()
    for copy in point_copies:
        copy.wait()
    here_rows = coupling_ref.shape[1]
    fine = points_all[...]

    def phases(lattice):
        winding = fine[:, 0:1] * lattice[0:1, :] + fine[:, 1:2] * lattice[1:2, :] + fine[:, 2:3] * lattice[2:3, :]
        winding = winding - NQG * jnp.floor((winding + 0.5) * (1.0 / NQG))
        angles = winding * (full_turn / NQG)
        weights = 1.0 / lattice[3:4, :]
        return (jnp.cos(angles) * weights)[:, :here_rows], (jnp.sin(angles) * weights)[:, :here_rows]

    own_real, own_imag = phases(lattice_ref[...])
    far_real, far_imag = phases(lattice_pair[...])
    left_real = jnp.concatenate([own_real, -own_imag, far_real, -far_imag], axis=1)
    left_imag = jnp.concatenate([own_imag, own_real, far_imag, far_real], axis=1)
    left = jnp.concatenate([left_real, left_imag], axis=0).astype(jnp.bfloat16)
    half = left_real.shape[0]

    load.wait()
    pair_copy.wait()
    columns = coupling_ref.shape[2]
    height = recv.shape[1]
    for first in range(0, columns, SPAN):
        count = min(SPAN, columns - first)
        block = rows_all[:, :, :, first : first + count].reshape(4 * here_rows, count)
        product = jnp.dot(left, block, preferred_element_type=jnp.float32)
        for begin in range(0, count, LANES):
            size = min(LANES, count - begin)
            piece = product[:, begin : begin + size]
            if size < LANES:
                piece = jnp.concatenate([piece, jnp.zeros((2 * half, LANES - size), jnp.float32)], axis=1)
            row = (first + begin) // LANES * 2
            for part in range(2):
                partial[pl.ds(row + part, half, stride=height), :] = piece[part * half : (part + 1) * half]

    source = partial
    if WIRE != jnp.float32:
        wire[...] = partial[...].astype(WIRE)
        source = wire

    copies = []
    for step in range(1, total):
        other, other_id = target(step)
        rows = pl.ds(pl.multiple_of(other * height, height), height)
        copy = pltpu.make_async_remote_copy(
            src_ref=source.at[rows, :], dst_ref=recv.at[step],
            send_sem=send_sem.at[step], recv_sem=recv_sem.at[step],
            device_id=other_id, device_id_type=MESH)
        copy.start()
        copies.append(copy)

    folded = partial[pl.ds(pl.multiple_of(me * height, height), height), :]
    for step in range(1, total):
        copies[step - 1].wait_recv()
        folded = folded + recv[step].astype(jnp.float32)
    for tile in range(flat.shape[1] // LANES):
        flat[:, tile * LANES : (tile + 1) * LANES] = folded[2 * tile : 2 * tile + 2]

    mode_count = modes_ref.shape[3]
    pairs = out_ref.shape[3]
    window = -(-(pairs + LANES // 2) // LANES) * LANES
    vectors_real = modes_ref[my_rp, 0]
    vectors_imag = modes_ref[my_rp, 1]
    moded_real = jnp.zeros((vectors_real.shape[0], pairs), jnp.float32)
    moded_imag = moded_real
    for a in range(mode_count):
        offset = a * pairs % LANES
        begin = a * pairs - offset
        value = flat[:, begin : begin + window]
        if offset:
            value = pltpu.roll(value, window - offset, 1)
        value = value[:, :pairs]
        fr, fi = value[0:1], value[1:2]
        vr, vi = vectors_real[:, a : a + 1], vectors_imag[:, a : a + 1]
        moded_real = moded_real + vr * fr - vi * fi
        moded_imag = moded_imag + vi * fr + vr * fi
    pad = moded_real.shape[0]
    high, low = split_wide(jnp.concatenate([moded_real, moded_imag], axis=0))
    both = jnp.concatenate([high, low], axis=0)

    def product(index):
        first = jnp.dot(both, kron[index], preferred_element_type=jnp.float32)
        second = jnp.dot(high, kron[index + 1], preferred_element_type=jnp.float32)
        return first[: 2 * pad] + first[2 * pad :] + second

    by_real = product(0)
    by_imag = product(2)
    out_ref[0, 0] = (by_real[:pad] - by_imag[pad:])[:mode_count]
    out_ref[0, 1] = (by_imag[:pad] + by_real[pad:])[:mode_count]
    for copy in copies:
        copy.wait_send()


def per_device(
    pool,
    rp,
    wannier_coupling,
    lattice_vectors,
    degeneracy,
    fine_points,
    mode_vectors,
    bands_shifted,
    bands_anchor,
):
    rows_here, columns = wannier_coupling.shape[1:]
    points = fine_points.shape[1]
    mode_count = mode_vectors.shape[2]
    pairs = columns // mode_count
    lattice = jnp.concatenate([lattice_vectors, degeneracy], axis=0).astype(jnp.float32)
    lattice = jnp.pad(lattice, ((0, 4), (0, LANES - rows_here)), constant_values=1.0)
    fine = jnp.pad(fine_points.astype(jnp.float32).T, ((0, 0), (0, LANES - 3)))
    pad_modes = -(-mode_count // 8) * 8
    modes = jnp.pad(jnp.swapaxes(mode_vectors, 2, 3), ((0, 0), (0, 0), (0, pad_modes - mode_count), (0, 0)))
    sides = pool // 2
    total = sides * rp
    tiles = -(-columns // LANES)
    height = -(-2 * tiles // 8) * 8
    vmem = pl.BlockSpec(memory_space=pltpu.VMEM)
    dma = pltpu.SemaphoreType.DMA
    return pl.pallas_call(
        functools.partial(kernel, pool, rp),
        out_shape=jax.ShapeDtypeStruct((1, 2, mode_count, pairs), jnp.float32),
        in_specs=[pl.BlockSpec(memory_space=pl.ANY)] + [vmem] * 5,
        out_specs=vmem,
        scratch_shapes=[
            pltpu.VMEM((2, 2, rows_here, columns), jnp.bfloat16),
            pltpu.VMEM(lattice.shape, jnp.float32),
            pltpu.VMEM((sides * points, LANES), jnp.float32),
            pltpu.VMEM((total * height, LANES), jnp.float32),
            pltpu.VMEM((total * height, LANES), WIRE) if WIRE != jnp.float32 else pltpu.VMEM((16, LANES), WIRE),
            pltpu.VMEM((total, height, LANES), WIRE),
            pltpu.VMEM((2, tiles * LANES), jnp.float32),
            pltpu.VMEM((4, pairs, pairs), jnp.bfloat16),
            dma, dma, dma, dma, dma,
            dma((sides - 1,)), dma((sides - 1,)),
            dma((total,)), dma((total,)),
        ],
        compiler_params=pltpu.CompilerParams(
            collective_id=0, has_side_effects=True, vmem_limit_bytes=48 * 1024 * 1024
        ),
    )(wannier_coupling, lattice, fine, modes, bands_shifted, bands_anchor)


def solution(mesh):
    return jax.shard_map(
        functools.partial(per_device, mesh.shape["pool"], mesh.shape["rp"]),
        mesh=mesh,
        in_specs=(
            P(None, ("pool", "rp"), None),
            P(None, ("pool", "rp")),
            P(None, ("pool", "rp")),
            P(None, "pool"),
            P("pool", None, None, None),
            P(("pool", "rp"), None, None, None),
            P(),
        ),
        out_specs=P(("pool", "rp"), None, None, None),
        check_vma=False,
    )
```

time: 131 us -> 27.9 us (0.21)
  the two profiles are of different devices: /device:TPU:0 before, /device:TPU:13 now
where the time goes in v1:
time: 27.9 us; the launch traced here: 27.7 us
  Pallas kernels  24.5 us (88%)
  local copies, waits for them, and re-layouts  3.12 us (11%)
    pallas_call x1, Pallas kernels, per_device(): pl.pallas_call(functools.partial(kernel, pool, rp), out_shape=jax.ShapeDt...  24.5 us
    unnamed x14, local copies, waits for them, and re-layouts  2.45 us
    pallas_call x1, local copies, waits for them, and re-layouts, per_device(): pl.pallas_call(functools.partial(kernel, pool, rp), out_shape=jax.ShapeDt...  0.64 us

profile of v1, /device:TPU:13, one launch (start us, length us, event | category | flops | bytes accessed | tf_op | source)
XLA Modules:
  0.0 27.7 jit_solution(17442962358755083093)
XLA Ops:
  0.0 0.0 copy-start
  0.0 1.1 %copy.9 = f32[8,2,9,9]{2,3,1,0:T(8,128)S(1)} copy(f32[8,2,9,9]{3,1,2,0:T(2,128)} %param.11) | data formatting | bytes 10368 | tf_op args[4]
  1.1 0.0 copy-start.3
  1.1 0.0 copy-start.4
  1.1 0.0 copy-start.5
  1.2 0.0 copy-start.2
  1.2 0.6 %copy-done.3 = s32[3,8]{1,0:T(4,128)S(1)} copy-done((s32[3,8]{1,0:T(4,128)S(1)}, s32[3,8]{1,0:T(4,128)}, u32[]{:S(2)}) %copy-start.3) | copy-done | bytes 120
  1.8 0.0 copy-start.1
  1.8 0.1 copy.8
  1.9 0.0 copy-done.4
  1.9 0.0 copy-done.5
  2.0 0.0 copy-done
  2.0 0.0 copy-done.2
  2.0 0.6 %copy-done.1 = f32[1,2,24,24]{3,2,1,0:T(8,128)S(1)} copy-done((f32[1,2,24,24]{3,2,1,0:T(8,128)S(1)}, f32[1,2,24,24]{3,2,1,0:T(8,128)}, u32[]{:S(2)}) %copy-start.1) | copy-done | bytes 4632
  2.6 24.5 %shard_map.73 = f32[1,2,9,576]{3,2,1,0:T(8,128)S(1)} custom-call(bf16[2,16,5184]{2,1,0:T(8,128)(2,1)S(1)} %copy-done, f32[8,128]{1,0:T(8,128)S(1)} %pad.12.lattice_ref, f32[8,128]{1,0:T(8,128)S(1)} %pad.13.points_ref, f32[8,2,16,9]{3,2,1,0:T(8,128)S(1)} %pad.14.modes_ref, f32[1,2,24,24]{3,2,1,0:T(8,128)S(1)} %copy-done.1, f32[2,24,24]{2,1,0:T(8,128)S(1)} %copy-done.2), custom_call_target="tpu_custom_call" | custom-call | tf_op jit(solution)/shard_map/pallas_call | solution.py:253
  27.0 0.6 %copy.10 = f32[1,2,9,576]{3,1,2,0:T(2,128)} copy(f32[1,2,9,576]{3,2,1,0:T(8,128)S(1)} %shard_map.73) | data formatting | bytes 82944 | tf_op jit(solution)/shard_map/pallas_call | solution.py:253
  (5 shorter events, 0.0 us)
Async XLA Ops:
  0.0 2.0 %copy-start = (bf16[2,16,5184]{2,1,0:T(8,128)(2,1)S(1)}, bf16[2,16,5184]{2,1,0:T(8,128)(2,1)}, u32[]{:S(2)}) copy-start(bf16[2,16,5184]{2,1,0:T(8,128)(2,1)} %coupling_ref.1) | copy-start | bytes 995332
  1.1 0.7 %copy-start.3 = (s32[3,8]{1,0:T(4,128)S(1)}, s32[3,8]{1,0:T(4,128)}, u32[]{:S(2)}) copy-start(s32[3,8]{1,0:T(4,128)} %param.10) | copy-start | bytes 292
  1.1 0.8 %copy-start.4 = (s32[3,16]{1,0:T(4,128)S(1)}, s32[3,16]{1,0:T(4,128)}, u32[]{:S(2)}) copy-start(s32[3,16]{1,0:T(4,128)} %param.8) | copy-start | bytes 580
  1.1 0.8 %copy-start.5 = (s32[1,16]{1,0:T(1,128)S(1)}, s32[1,16]{1,0:T(1,128)}, u32[]{:S(2)}) copy-start(s32[1,16]{1,0:T(1,128)} %param.9) | copy-start | bytes 196
  1.2 0.8 %copy-start.2 = (f32[2,24,24]{2,1,0:T(8,128)S(1)}, f32[2,24,24]{2,1,0:T(8,128)}, u32[]{:S(2)}) copy-start(f32[2,24,24]{2,1,0:T(8,128)} %anchor_ref.1) | copy-start | bytes 13828
  1.8 0.7 %copy-start.1 = (f32[1,2,24,24]{3,2,1,0:T(8,128)S(1)}, f32[1,2,24,24]{3,2,1,0:T(8,128)}, u32[]{:S(2)}) copy-start(f32[1,2,24,24]{3,2,1,0:T(8,128)} %shifted_ref.1) | copy-start | bytes 13828

commit v2 on v1

v2 whole, which is shorter than its diff:
```python
import functools
import math

import jax
import jax.numpy as jnp
from jax import lax
from jax.experimental import pallas as pl
from jax.experimental.pallas import tpu as pltpu
from jax.sharding import PartitionSpec as P

NQG = 48
LANES = 128
SPAN = 1024
WIRE = jnp.int16
TOP = 32000.0

full_turn = 2.0 * math.pi
highest = lax.Precision.HIGHEST
MESH = pl.DeviceIdType.MESH


def split_wide(value):
    high = value.astype(jnp.bfloat16)
    low = (value - high.astype(jnp.float32)).astype(jnp.bfloat16)
    return high, low


def build_pairs(shifted_ref, anchor_ref, kron):
    bands = anchor_ref.shape[1]
    pairs = bands * bands
    row = lax.broadcasted_iota(jnp.int32, (bands, pairs), 0).astype(jnp.float32)
    col = lax.broadcasted_iota(jnp.int32, (bands, pairs), 1).astype(jnp.float32)
    outer = jnp.floor((col + 0.5) * (1.0 / bands))
    inner = col - outer * bands
    pick_outer = jnp.where(row == outer, 1.0, 0.0)
    pick_inner = jnp.where(row == inner, 1.0, 0.0)

    def spread(matrix, pick):
        return jnp.dot(matrix, pick, precision=highest, preferred_element_type=jnp.float32)

    shift_real = spread(shifted_ref[0, 0], pick_outer)
    shift_imag = spread(shifted_ref[0, 1], pick_outer)
    anchor_real = spread(anchor_ref[0], pick_inner)
    anchor_imag = spread(anchor_ref[1], pick_inner)
    for start in range(0, bands, 2):
        reals, imags = [], []
        for m in (start, start + 1):
            sr = shift_real[m : m + 1]
            si = shift_imag[m : m + 1]
            reals.append(sr * anchor_real + si * anchor_imag)
            imags.append(sr * anchor_imag - si * anchor_real)
        rows = pl.ds(start * bands, 2 * bands)
        kron[0, rows, :], kron[1, rows, :] = split_wide(jnp.concatenate(reals, axis=0))
        kron[2, rows, :], kron[3, rows, :] = split_wide(jnp.concatenate(imags, axis=0))


def far_first(sides, rp):
    shifts = sorted(range(rp), key=lambda shift: -min(shift, rp - shift))
    return [(side, shift) for shift in shifts for side in reversed(range(sides)) if side or shift]


def kernel(
    pool,
    rp,
    coupling_ref,
    lattice_ref,
    weight_ref,
    points_ref,
    modes_ref,
    shifted_ref,
    anchor_ref,
    out_ref,
    rows_all,
    lattice,
    weight,
    points,
    modes,
    shifted,
    anchor,
    partial,
    wire,
    recv,
    flat,
    kron,
    load_sem,
    pair_send,
    pair_recv,
    point_send,
    point_recv,
    send_sem,
    recv_sem,
):
    sides = pool // 2
    my_pool = lax.axis_index("pool")
    my_rp = lax.axis_index("rp")
    core = lax.rem(my_pool, 2)
    side = my_pool // 2
    partner = side * 2 + 1 - core
    total = sides * rp
    order = far_first(sides, rp)
    pair_id = {"pool": partner, "rp": my_rp}

    def target(step):
        other_side = lax.rem(side + step[0], sides)
        other_rp = lax.rem(my_rp + step[1], rp)
        return other_side * rp + other_rp, {"pool": other_side * 2 + core, "rp": other_rp}

    barrier = pltpu.get_barrier_semaphore()
    for step in order:
        pl.semaphore_signal(barrier, inc=1, device_id=target(step)[1], device_id_type=MESH)
    pl.semaphore_signal(barrier, inc=1, device_id=pair_id, device_id_type=MESH)

    loads = []
    for number, (source, place) in enumerate((
        (coupling_ref, rows_all.at[0]),
        (lattice_ref, lattice.at[0]),
        (weight_ref, weight.at[0]),
        (points_ref, points.at[side]),
        (modes_ref.at[my_rp], modes),
        (shifted_ref, shifted),
        (anchor_ref, anchor),
    )):
        load = pltpu.make_async_copy(source, place, load_sem.at[number])
        load.start()
        loads.append(load)
    loads[5].wait()
    loads[6].wait()
    build_pairs(shifted, anchor, kron)
    for load in loads[:5]:
        load.wait()

    pl.semaphore_wait(barrier, total)

    copies = []
    for number, place in enumerate((lattice, weight, rows_all)):
        copy = pltpu.make_async_remote_copy(
            src_ref=place.at[0], dst_ref=place.at[1], send_sem=pair_send.at[number], recv_sem=pair_recv.at[number],
            device_id=pair_id, device_id_type=MESH)
        copy.start()
        copies.append(copy)
    for step in range(1, sides):
        other_side = lax.rem(side + step, sides)
        copy = pltpu.make_async_remote_copy(
            src_ref=points.at[side], dst_ref=points.at[side],
            send_sem=point_send.at[step - 1], recv_sem=point_recv.at[step - 1],
            device_id={"pool": other_side * 2 + core, "rp": my_rp}, device_id_type=MESH)
        copy.start()
        copies.append(copy)
    for copy in copies[:2] + copies[3:]:
        copy.wait()
    here_rows = coupling_ref.shape[1]

    def turn(left, right):
        return lax.dot_general(left, right, (((0,), (0,)), ((), ())), precision=highest, preferred_element_type=jnp.float32)

    def phases(which):
        vectors = lattice[which].astype(jnp.float32)
        winding = jnp.concatenate([turn(points[s].astype(jnp.float32), vectors) for s in range(sides)], axis=0)
        winding = jnp.floor(winding + 0.5)
        winding = winding - NQG * jnp.floor((winding + 0.5) * (1.0 / NQG))
        angles = winding * (full_turn / NQG)
        weights = 1.0 / weight[which].astype(jnp.float32)
        return jnp.cos(angles) * weights, jnp.sin(angles) * weights

    own_real, own_imag = phases(0)
    far_real, far_imag = phases(1)
    left_real = jnp.concatenate([own_real, -own_imag, far_real, -far_imag], axis=1)
    left_imag = jnp.concatenate([own_imag, own_real, far_imag, far_real], axis=1)
    left = jnp.concatenate([left_real, left_imag], axis=0).astype(jnp.bfloat16)
    half = left_real.shape[0]

    copies[2].wait()
    columns = coupling_ref.shape[2]
    height = recv.shape[1]
    largest = jnp.full((half, LANES), 1e-30, jnp.float32)
    for first in range(0, columns, SPAN):
        count = min(SPAN, columns - first)
        block = rows_all[:, :, :, first : first + count].reshape(4 * here_rows, count)
        product = jnp.dot(left, block, preferred_element_type=jnp.float32)
        for begin in range(0, count, LANES):
            size = min(LANES, count - begin)
            piece = product[:, begin : begin + size]
            if size < LANES:
                piece = jnp.concatenate([piece, jnp.zeros((2 * half, LANES - size), jnp.float32)], axis=1)
            row = (first + begin) // LANES * 2
            largest = jnp.maximum(largest, jnp.maximum(jnp.abs(piece[:half]), jnp.abs(piece[half:])))
            for part in range(2):
                partial[pl.ds(row + part, half, stride=height), :] = piece[part * half : (part + 1) * half]

    used = 2 * (-(-columns // LANES))
    largest = jnp.max(jnp.max(largest, axis=0, keepdims=True), axis=1, keepdims=True)
    exponent = jnp.ceil(jnp.log2(largest * (1.0 / TOP)) + 1e-3)
    inverse = jnp.broadcast_to(jnp.exp2(-exponent), (1, LANES))
    exponent = jnp.broadcast_to(exponent, (height, LANES))
    is_value = lax.broadcasted_iota(jnp.int32, (height, LANES), 0) < used

    copies = []
    for number, step in enumerate(order):
        other, other_id = target(step)
        rows = pl.ds(pl.multiple_of(other * height, 8), height)
        coded = jnp.where(is_value, partial[rows, :] * inverse, exponent)
        wire[number] = jnp.round(coded).astype(jnp.int32).astype(WIRE)
        copies.append(pltpu.make_async_remote_copy(
            src_ref=wire.at[number], dst_ref=recv.at[number],
            send_sem=send_sem.at[number], recv_sem=recv_sem.at[number],
            device_id=other_id, device_id_type=MESH))
        if number:
            copies[number - 1].start()
    copies[-1].start()

    me = side * rp + my_rp
    folded = partial[pl.ds(pl.multiple_of(me * height, 8), height), :]
    for number in reversed(range(len(order))):
        copies[number].wait_recv()
        coded = recv[number].astype(jnp.int32).astype(jnp.float32)
        folded = folded + coded * jnp.exp2(coded[used : used + 1])
    for tile in range(flat.shape[1] // LANES):
        flat[:, tile * LANES : (tile + 1) * LANES] = folded[2 * tile : 2 * tile + 2]

    mode_count = modes_ref.shape[3]
    pad = -(-mode_count // 8) * 8
    pairs = out_ref.shape[3]
    window = -(-(pairs + LANES // 2) // LANES) * LANES
    unit_row = lax.broadcasted_iota(jnp.int32, (mode_count, LANES), 0)
    unit_col = lax.broadcasted_iota(jnp.int32, (mode_count, LANES), 1)
    unit = jnp.where(unit_row == unit_col, 1.0, 0.0)
    empty = jnp.zeros((pad - mode_count, LANES), jnp.float32)
    vectors_real = jnp.concatenate([turn(modes[0], unit), empty], axis=0)
    vectors_imag = jnp.concatenate([turn(modes[1], unit), empty], axis=0)
    moded_real = jnp.zeros((vectors_real.shape[0], pairs), jnp.float32)
    moded_imag = moded_real
    for a in range(mode_count):
        offset = a * pairs % LANES
        begin = a * pairs - offset
        value = flat[:, begin : begin + window]
        if offset:
            value = pltpu.roll(value, window - offset, 1)
        value = value[:, :pairs]
        fr, fi = value[0:1], value[1:2]
        vr, vi = vectors_real[:, a : a + 1], vectors_imag[:, a : a + 1]
        moded_real = moded_real + vr * fr - vi * fi
        moded_imag = moded_imag + vi * fr + vr * fi
    high, low = split_wide(jnp.concatenate([moded_real, moded_imag], axis=0))
    both = jnp.concatenate([high, low], axis=0)

    def product(index):
        first = jnp.dot(both, kron[index], preferred_element_type=jnp.float32)
        second = jnp.dot(high, kron[index + 1], preferred_element_type=jnp.float32)
        return first[: 2 * pad] + first[2 * pad :] + second

    by_real = product(0)
    by_imag = product(2)
    out_ref[0, 0] = (by_real[:pad] - by_imag[pad:])[:mode_count]
    out_ref[0, 1] = (by_imag[:pad] + by_real[pad:])[:mode_count]
    for copy in copies:
        copy.wait_send()


def per_device(
    pool,
    rp,
    wannier_coupling,
    lattice_vectors,
    degeneracy,
    fine_points,
    mode_vectors,
    bands_shifted,
    bands_anchor,
):
    rows_here, columns = wannier_coupling.shape[1:]
    points = fine_points.shape[1]
    mode_count = mode_vectors.shape[2]
    pairs = columns // mode_count
    sides = pool // 2
    total = sides * rp
    tiles = -(-columns // LANES)
    height = -(-(2 * tiles + 1) // 8) * 8
    dma = pltpu.SemaphoreType.DMA
    return pl.pallas_call(
        functools.partial(kernel, pool, rp),
        out_shape=jax.ShapeDtypeStruct((1, 2, mode_count, pairs), jnp.float32),
        in_specs=[pl.BlockSpec(memory_space=pl.ANY)] * 7,
        out_specs=pl.BlockSpec(memory_space=pltpu.VMEM),
        scratch_shapes=[
            pltpu.VMEM((2, 2, rows_here, columns), jnp.bfloat16),
            pltpu.VMEM((2, 3, rows_here), jnp.int32),
            pltpu.VMEM((2, 1, rows_here), jnp.int32),
            pltpu.VMEM((sides, 3, points), jnp.int32),
            pltpu.VMEM(mode_vectors.shape[1:], jnp.float32),
            pltpu.VMEM(bands_shifted.shape, jnp.float32),
            pltpu.VMEM(bands_anchor.shape, jnp.float32),
            pltpu.VMEM((total * height, LANES), jnp.float32),
            pltpu.VMEM((total - 1, height, LANES), WIRE),
            pltpu.VMEM((total - 1, height, LANES), WIRE),
            pltpu.VMEM((2, tiles * LANES), jnp.float32),
            pltpu.VMEM((4, pairs, pairs), jnp.bfloat16),
            dma((7,)), dma((3,)), dma((3,)),
            dma((sides - 1,)), dma((sides - 1,)),
            dma((total - 1,)), dma((total - 1,)),
        ],
        compiler_params=pltpu.CompilerParams(
            collective_id=0, has_side_effects=True, vmem_limit_bytes=48 * 1024 * 1024
        ),
    )(wannier_coupling, lattice_vectors, degeneracy, fine_points, mode_vectors, bands_shifted, bands_anchor)


def solution(mesh):
    return jax.shard_map(
        functools.partial(per_device, mesh.shape["pool"], mesh.shape["rp"]),
        mesh=mesh,
        in_specs=(
            P(None, ("pool", "rp"), None),
            P(None, ("pool", "rp")),
            P(None, ("pool", "rp")),
            P(None, "pool"),
            P("pool", None, None, None),
            P(("pool", "rp"), None, None, None),
            P(),
        ),
        out_specs=P(("pool", "rp"), None, None, None),
        check_vma=False,
    )
```

time: 27.9 us -> 21.4 us (0.77)
  the two profiles are of different devices: /device:TPU:13 before, /device:TPU:0 now
where the time goes in v2:
time: 21.4 us; the launch traced here: 21.2 us
  Pallas kernels  18.6 us (87%)
  local copies, waits for them, and re-layouts  2.6 us (12%)
    pallas_call x1, Pallas kernels, per_device(): pl.pallas_call(functools.partial(kernel, pool, rp), out_shape=jax.ShapeDt...  18.6 us
    unnamed x13, local copies, waits for them, and re-layouts  1.95 us
    pallas_call x1, local copies, waits for them, and re-layouts, per_device(): pl.pallas_call(functools.partial(kernel, pool, rp), out_shape=jax.ShapeDt...  0.64 us

profile of v2, /device:TPU:0, one launch (start us, length us, event | category | flops | bytes accessed | tf_op | source)
XLA Modules:
  0.0 21.2 jit_solution(3170558094861979224)
XLA Ops:
  0.0 0.0 copy-start.2
  0.0 0.0 copy-start.1
  0.0 0.0 copy-start.4
  0.0 0.0 copy-start.5
  0.0 0.0 copy-start.3
  0.0 1.0 %copy.8.modes_ref = f32[8,2,9,9]{3,2,1,0:T(8,128)S(1)} copy(f32[8,2,9,9]{3,1,2,0:T(2,128)} %param.11) | data formatting | bytes 10368 | tf_op args[4]
  1.0 0.0 copy-done.2
  1.0 0.0 copy-done.1
  1.0 0.0 copy-done.4
  1.0 0.0 copy-done.5
  1.0 0.0 copy-done.3
  1.0 0.0 copy-start
  1.0 1.0 %copy-done = bf16[2,16,5184]{2,1,0:T(8,128)(2,1)S(1)} copy-done((bf16[2,16,5184]{2,1,0:T(8,128)(2,1)S(1)}, bf16[2,16,5184]{2,1,0:T(8,128)(2,1)}, u32[]{:S(2)}) %copy-start) | copy-done | bytes 331800
  2.0 18.6 %shard_map.73 = f32[1,2,9,576]{3,2,1,0:T(8,128)S(1)} custom-call(bf16[2,16,5184]{2,1,0:T(8,128)(2,1)S(1)} %copy-done, s32[3,16]{1,0:T(4,128)S(1)} %copy-done.3, s32[1,16]{1,0:T(1,128)S(1)} %copy-done.5, s32[3,8]{1,0:T(4,128)S(1)} %copy-done.4, f32[8,2,9,9]{3,2,1,0:T(8,128)S(1)} %copy.8.modes_ref, f32[1,2,24,24]{3,2,1,0:T(8,128)S(1)} %copy-done.1, ...), custom_call_target="tpu_custom_call" | custom-call | tf_op jit(solution)/shard_map/pallas_call | solution.py:279
  20.6 0.6 %copy.9 = f32[1,2,9,576]{3,1,2,0:T(2,128)} copy(f32[1,2,9,576]{3,2,1,0:T(8,128)S(1)} %shard_map.73) | data formatting | bytes 82944 | tf_op jit(solution)/shard_map/pallas_call | solution.py:279
Async XLA Ops:
  0.0 1.0 %copy-start.2 = (f32[2,24,24]{2,1,0:T(8,128)S(1)}, f32[2,24,24]{2,1,0:T(8,128)}, u32[]{:S(2)}) copy-start(f32[2,24,24]{2,1,0:T(8,128)} %anchor_ref.1) | copy-start | bytes 13828
  0.0 1.0 %copy-start.1 = (f32[1,2,24,24]{3,2,1,0:T(8,128)S(1)}, f32[1,2,24,24]{3,2,1,0:T(8,128)}, u32[]{:S(2)}) copy-start(f32[1,2,24,24]{3,2,1,0:T(8,128)} %shifted_ref.1) | copy-start | bytes 13828
  0.0 1.0 %copy-start.4 = (s32[3,8]{1,0:T(4,128)S(1)}, s32[3,8]{1,0:T(4,128)}, u32[]{:S(2)}) copy-start(s32[3,8]{1,0:T(4,128)} %points_ref.1) | copy-start | bytes 292
  0.0 1.0 %copy-start.5 = (s32[1,16]{1,0:T(1,128)S(1)}, s32[1,16]{1,0:T(1,128)}, u32[]{:S(2)}) copy-start(s32[1,16]{1,0:T(1,128)} %weight_ref.1) | copy-start | bytes 196
  0.0 1.0 %copy-start.3 = (s32[3,16]{1,0:T(4,128)S(1)}, s32[3,16]{1,0:T(4,128)}, u32[]{:S(2)}) copy-start(s32[3,16]{1,0:T(4,128)} %lattice_ref.1) | copy-start | bytes 580
  1.0 1.0 %copy-start = (bf16[2,16,5184]{2,1,0:T(8,128)(2,1)S(1)}, bf16[2,16,5184]{2,1,0:T(8,128)(2,1)}, u32[]{:S(2)}) copy-start(bf16[2,16,5184]{2,1,0:T(8,128)(2,1)} %coupling_ref.1) | copy-start | bytes 995332

commit v3 on v2

--- a/solution.py
+++ b/solution.py
@@ -54,9 +54,13 @@
         kron[2, rows, :], kron[3, rows, :] = split_wide(jnp.concatenate(imags, axis=0))
 
 
-def far_first(sides, rp):
-    shifts = sorted(range(rp), key=lambda shift: -min(shift, rp - shift))
-    return [(side, shift) for shift in shifts for side in reversed(range(sides)) if side or shift]
+def split_chain(rp):
+    low = 1
+    while low * low * 4 <= rp:
+        low *= 2
+    while rp % low:
+        low -= 1
+    return rp // low, low
 
 
 def kernel(
@@ -80,6 +84,8 @@
     partial,
     wire,
     recv,
+    chain_wire,
+    chain_in,
     flat,
     kron,
     load_sem,
@@ -87,8 +93,10 @@
     pair_recv,
     point_send,
     point_recv,
-    send_sem,
-    recv_sem,
+    plane_send,
+    plane_recv,
+    chain_send,
+    chain_recv,
 ):
     sides = pool // 2
     my_pool = lax.axis_index("pool")
@@ -96,18 +104,30 @@
     core = lax.rem(my_pool, 2)
     side = my_pool // 2
     partner = side * 2 + 1 - core
-    total = sides * rp
-    order = far_first(sides, rp)
+    high_count, low_count = split_chain(rp)
+    high, low = my_rp // low_count, lax.rem(my_rp, low_count)
+    peers = [(s, shift) for s in range(sides) for shift in range(low_count) if s or shift]
+    shifts = sorted(range(high_count), key=lambda shift: -min(shift, high_count - shift))
     pair_id = {"pool": partner, "rp": my_rp}
 
-    def target(step):
-        other_side = lax.rem(side + step[0], sides)
-        other_rp = lax.rem(my_rp + step[1], rp)
-        return other_side * rp + other_rp, {"pool": other_side * 2 + core, "rp": other_rp}
+    def slab_of(other_side, other_high, other_low):
+        return (other_side * high_count + other_high) * low_count + other_low
+
+    def plane_peer(step):
+        return lax.rem(side + step[0], sides), lax.rem(low + step[1], low_count)
+
+    def device(other_side, other_high, other_low):
+        return {"pool": other_side * 2 + core, "rp": other_high * low_count + other_low}
+
+    def chain_peer(shift):
+        return lax.rem(high + shift, high_count)
 
     barrier = pltpu.get_barrier_semaphore()
-    for step in order:
-        pl.semaphore_signal(barrier, inc=1, device_id=target(step)[1], device_id_type=MESH)
+    for shift in shifts[:-1]:
+        pl.semaphore_signal(barrier, inc=1, device_id=device(side, chain_peer(shift), low), device_id_type=MESH)
+    for step in peers:
+        other_side, other_low = plane_peer(step)
+        pl.semaphore_signal(barrier, inc=1, device_id=device(other_side, high, other_low), device_id_type=MESH)
     pl.semaphore_signal(barrier, inc=1, device_id=pair_id, device_id_type=MESH)
 
     loads = []
@@ -129,7 +149,7 @@
     for load in loads[:5]:
         load.wait()
 
-    pl.semaphore_wait(barrier, total)
+    pl.semaphore_wait(barrier, len(peers) + high_count)
 
     copies = []
     for number, place in enumerate((lattice, weight, rows_all)):
@@ -194,30 +214,58 @@
     exponent = jnp.broadcast_to(exponent, (height, LANES))
     is_value = lax.broadcasted_iota(jnp.int32, (height, LANES), 0) < used
 
+    def slab(index):
+        return partial[pl.ds(pl.multiple_of(index * height, 8), height), :]
+
+    def code(values, scale, powers):
+        return jnp.round(jnp.where(is_value, values * scale, powers)).astype(jnp.int32).astype(WIRE)
+
     copies = []
-    for number, step in enumerate(order):
-        other, other_id = target(step)
-        rows = pl.ds(pl.multiple_of(other * height, 8), height)
-        coded = jnp.where(is_value, partial[rows, :] * inverse, exponent)
-        wire[number] = jnp.round(coded).astype(jnp.int32).astype(WIRE)
-        copies.append(pltpu.make_async_remote_copy(
-            src_ref=wire.at[number], dst_ref=recv.at[number],
-            send_sem=send_sem.at[number], recv_sem=recv_sem.at[number],
-            device_id=other_id, device_id_type=MESH))
-        if number:
-            copies[number - 1].start()
+    for shift in shifts:
+        other_high = chain_peer(shift)
+        for step in peers:
+            number = len(copies)
+            other_side, other_low = plane_peer(step)
+            wire[number] = code(slab(slab_of(other_side, other_high, other_low)), inverse, exponent)
+            copies.append(pltpu.make_async_remote_copy(
+                src_ref=wire.at[number], dst_ref=recv.at[number],
+                send_sem=plane_send.at[number], recv_sem=plane_recv.at[number],
+                device_id=device(other_side, high, other_low), device_id_type=MESH))
+            if number:
+                copies[number - 1].start()
     copies[-1].start()
 
-    me = side * rp + my_rp
-    folded = partial[pl.ds(pl.multiple_of(me * height, 8), height), :]
-    for number in reversed(range(len(order))):
-        copies[number].wait_recv()
-        coded = recv[number].astype(jnp.int32).astype(jnp.float32)
+    room = (len(peers)).bit_length()
+    plane_copies = list(copies)
+    chain_copies = []
+    for place, shift in enumerate(shifts):
+        other_high = chain_peer(shift)
+        folded = slab(slab_of(side, other_high, low))
+        widest = exponent[:1]
+        for number in range(place * len(peers), (place + 1) * len(peers)):
+            plane_copies[number].wait_recv()
+            coded = recv[number].astype(jnp.int32).astype(jnp.float32)
+            power = coded[used : used + 1]
+            widest = jnp.maximum(widest, power)
+            folded = folded + coded * jnp.exp2(power)
+        if shift:
+            powers = widest + room
+            chain_wire[place] = code(folded, jnp.exp2(-powers), jnp.broadcast_to(powers, (height, LANES)))
+            copy = pltpu.make_async_remote_copy(
+                src_ref=chain_wire.at[place], dst_ref=chain_in.at[place],
+                send_sem=chain_send.at[place], recv_sem=chain_recv.at[place],
+                device_id=device(side, other_high, low), device_id_type=MESH)
+            copy.start()
+            chain_copies.append(copy)
+    for place, copy in enumerate(chain_copies):
+        copy.wait_recv()
+        coded = chain_in[place].astype(jnp.int32).astype(jnp.float32)
         folded = folded + coded * jnp.exp2(coded[used : used + 1])
+    copies = plane_copies + chain_copies
     for tile in range(flat.shape[1] // LANES):
         flat[:, tile * LANES : (tile + 1) * LANES] = folded[2 * tile : 2 * tile + 2]
 
-    mode_count = modes_ref.shape[3]
+    mode_count = modes_ref.shape[1]
     pad = -(-mode_count // 8) * 8
     pairs = out_ref.shape[3]
     window = -(-(pairs + LANES // 2) // LANES) * LANES
@@ -225,8 +273,8 @@
     unit_col = lax.broadcasted_iota(jnp.int32, (mode_count, LANES), 1)
     unit = jnp.where(unit_row == unit_col, 1.0, 0.0)
     empty = jnp.zeros((pad - mode_count, LANES), jnp.float32)
-    vectors_real = jnp.concatenate([turn(modes[0], unit), empty], axis=0)
-    vectors_imag = jnp.concatenate([turn(modes[1], unit), empty], axis=0)
+    vectors_real = jnp.concatenate([turn(modes[:, 0, :], unit), empty], axis=0)
+    vectors_imag = jnp.concatenate([turn(modes[:, 1, :], unit), empty], axis=0)
     moded_real = jnp.zeros((vectors_real.shape[0], pairs), jnp.float32)
     moded_imag = moded_real
     for a in range(mode_count):
@@ -240,18 +288,18 @@
         vr, vi = vectors_real[:, a : a + 1], vectors_imag[:, a : a + 1]
         moded_real = moded_real + vr * fr - vi * fi
         moded_imag = moded_imag + vi * fr + vr * fi
-    high, low = split_wide(jnp.concatenate([moded_real, moded_imag], axis=0))
-    both = jnp.concatenate([high, low], axis=0)
+    coarse, rest = split_wide(jnp.concatenate([moded_real, moded_imag], axis=0))
+    both = jnp.concatenate([coarse, rest], axis=0)
 
     def product(index):
         first = jnp.dot(both, kron[index], preferred_element_type=jnp.float32)
-        second = jnp.dot(high, kron[index + 1], preferred_element_type=jnp.float32)
+        second = jnp.dot(coarse, kron[index + 1], preferred_element_type=jnp.float32)
         return first[: 2 * pad] + first[2 * pad :] + second
 
     by_real = product(0)
     by_imag = product(2)
-    out_ref[0, 0] = (by_real[:pad] - by_imag[pad:])[:mode_count]
-    out_ref[0, 1] = (by_imag[:pad] + by_real[pad:])[:mode_count]
+    out_ref[0, :, 0, :] = (by_real[:pad] - by_imag[pad:])[:mode_count]
+    out_ref[0, :, 1, :] = (by_imag[:pad] + by_real[pad:])[:mode_count]
     for copy in copies:
         copy.wait_send()
 
@@ -276,9 +324,11 @@
     tiles = -(-columns // LANES)
     height = -(-(2 * tiles + 1) // 8) * 8
     dma = pltpu.SemaphoreType.DMA
-    return pl.pallas_call(
+    high_count, low_count = split_chain(rp)
+    plane = high_count * (sides * low_count - 1)
+    result = pl.pallas_call(
         functools.partial(kernel, pool, rp),
-        out_shape=jax.ShapeDtypeStruct((1, 2, mode_count, pairs), jnp.float32),
+        out_shape=jax.ShapeDtypeStruct((1, mode_count, 2, pairs), jnp.float32),
         in_specs=[pl.BlockSpec(memory_space=pl.ANY)] * 7,
         out_specs=pl.BlockSpec(memory_space=pltpu.VMEM),
         scratch_shapes=[
@@ -286,22 +336,26 @@
             pltpu.VMEM((2, 3, rows_here), jnp.int32),
             pltpu.VMEM((2, 1, rows_here), jnp.int32),
             pltpu.VMEM((sides, 3, points), jnp.int32),
-            pltpu.VMEM(mode_vectors.shape[1:], jnp.float32),
+            pltpu.VMEM((mode_count, 2, mode_count), jnp.float32),
             pltpu.VMEM(bands_shifted.shape, jnp.float32),
             pltpu.VMEM(bands_anchor.shape, jnp.float32),
             pltpu.VMEM((total * height, LANES), jnp.float32),
-            pltpu.VMEM((total - 1, height, LANES), WIRE),
-            pltpu.VMEM((total - 1, height, LANES), WIRE),
+            pltpu.VMEM((plane, height, LANES), WIRE),
+            pltpu.VMEM((plane, height, LANES), WIRE),
+            pltpu.VMEM((high_count - 1, height, LANES), WIRE),
+            pltpu.VMEM((high_count - 1, height, LANES), WIRE),
             pltpu.VMEM((2, tiles * LANES), jnp.float32),
             pltpu.VMEM((4, pairs, pairs), jnp.bfloat16),
             dma((7,)), dma((3,)), dma((3,)),
             dma((sides - 1,)), dma((sides - 1,)),
-            dma((total - 1,)), dma((total - 1,)),
+            dma((plane,)), dma((plane,)),
+            dma((high_count - 1,)), dma((high_count - 1,)),
         ],
         compiler_params=pltpu.CompilerParams(
-            collective_id=0, has_side_effects=True, vmem_limit_bytes=48 * 1024 * 1024
+            collective_id=0, has_side_effects=True, vmem_limit_bytes=67043328
         ),
-    )(wannier_coupling, lattice_vectors, degeneracy, fine_points, mode_vectors, bands_shifted, bands_anchor)
+    )(wannier_coupling, lattice_vectors, degeneracy, fine_points, jnp.swapaxes(mode_vectors, 1, 2), bands_shifted, bands_anchor)
+    return jnp.swapaxes(result, 1, 2)
 
 
 def solution(mesh):

time: 21.4 us -> 20.8 us (0.972)
  local copies, waits for them, and re-layouts: 2.6 us -> 1.42 us
  Pallas kernels: 18.6 us -> 19.2 us
    pallas_call x1 -> x0, local copies, waits for them, and re-layouts: 0.64 us -> none  [per_device(): pl.pallas_call(functools.partial(kernel, pool, rp), out_shape=jax.ShapeDt...]
    pallas_call x1, Pallas kernels: 18.6 us -> 19.2 us  [per_device(): pl.pallas_call(functools.partial(kernel, pool, rp), out_shape=jax.ShapeDt...]
    unnamed x13 -> x1, local copies, waits for them, and re-layouts: 1.95 us -> 1.42 us
where the time goes in v3:
time: 20.8 us; the launch traced here: 20.6 us
  Pallas kernels  19.2 us (92%)
  local copies, waits for them, and re-layouts  1.42 us (7%)
    pallas_call x1, Pallas kernels, per_device(): pl.pallas_call(functools.partial(kernel, pool, rp), out_shape=jax.ShapeDt...  19.2 us
    unnamed x1, local copies, waits for them, and re-layouts  1.42 us

profile of v3, /device:TPU:0, one launch (start us, length us, event | category | flops | bytes accessed | tf_op | source)
XLA Modules:
  0.0 20.6 jit_solution(18353242841576160880)
XLA Ops:
  0.0 19.2 %shard_map.73 = f32[1,9,2,576]{3,2,1,0:T(2,128)} custom-call(bf16[2,16,5184]{2,1,0:T(8,128)(2,1)} %coupling_ref.1, s32[3,16]{1,0:T(4,128)} %lattice_ref.1, s32[1,16]{1,0:T(1,128)} %weight_ref.1, s32[3,8]{1,0:T(4,128)} %points_ref.1, f32[8,9,2,9]{3,2,1,0:T(2,128)} %bitcast.3, f32[1,2,24,24]{3,2,1,0:T(8,128)} %shifted_ref.1, f32[2,24,24]{2,1,0:T(8,128)} %anchor_ref.1), custom_call_target="tpu_custom_call" | custom-call | tf_op jit(solution)/shard_map/pallas_call | solution.py:329
  19.2 1.4 %copy.9 = f32[1,2,9,576]{3,1,2,0:T(2,128)} copy(f32[1,2,9,576]{3,1,2,0:T(2,128)} %bitcast.2) | data formatting | bytes 82944

commit v4 on v3

--- a/solution.py
+++ b/solution.py
@@ -152,12 +152,6 @@
     pl.semaphore_wait(barrier, len(peers) + high_count)
 
     copies = []
-    for number, place in enumerate((lattice, weight, rows_all)):
-        copy = pltpu.make_async_remote_copy(
-            src_ref=place.at[0], dst_ref=place.at[1], send_sem=pair_send.at[number], recv_sem=pair_recv.at[number],
-            device_id=pair_id, device_id_type=MESH)
-        copy.start()
-        copies.append(copy)
     for step in range(1, sides):
         other_side = lax.rem(side + step, sides)
         copy = pltpu.make_async_remote_copy(
@@ -166,7 +160,13 @@
             device_id={"pool": other_side * 2 + core, "rp": my_rp}, device_id_type=MESH)
         copy.start()
         copies.append(copy)
-    for copy in copies[:2] + copies[3:]:
+    for number, place in enumerate((lattice, weight, rows_all)):
+        copy = pltpu.make_async_remote_copy(
+            src_ref=place.at[0], dst_ref=place.at[1], send_sem=pair_send.at[number], recv_sem=pair_recv.at[number],
+            device_id=pair_id, device_id_type=MESH)
+        copy.start()
+        copies.append(copy)
+    for copy in copies[:-1]:
         copy.wait()
     here_rows = coupling_ref.shape[1]
 
@@ -189,7 +189,7 @@
     left = jnp.concatenate([left_real, left_imag], axis=0).astype(jnp.bfloat16)
     half = left_real.shape[0]
 
-    copies[2].wait()
+    copies[-1].wait()
     columns = coupling_ref.shape[2]
     height = recv.shape[1]
     largest = jnp.full((half, LANES), 1e-30, jnp.float32)

time: 20.8 us -> 20.8 us (level)
  no operation moved by 1% of the time
where the time goes in v4:
time: 20.8 us; the launch traced here: 20.6 us
  Pallas kernels  19.2 us (92%)
  local copies, waits for them, and re-layouts  1.42 us (7%)
    pallas_call x1, Pallas kernels, per_device(): pl.pallas_call(functools.partial(kernel, pool, rp), out_shape=jax.ShapeDt...  19.2 us
    unnamed x1, local copies, waits for them, and re-layouts  1.42 us

profile of v4, /device:TPU:0, one launch (start us, length us, event | category | flops | bytes accessed | tf_op | source)
XLA Modules:
  0.0 20.6 jit_solution(10746662777842615178)
XLA Ops:
  0.0 19.2 %shard_map.73 = f32[1,9,2,576]{3,2,1,0:T(2,128)} custom-call(bf16[2,16,5184]{2,1,0:T(8,128)(2,1)} %coupling_ref.1, s32[3,16]{1,0:T(4,128)} %lattice_ref.1, s32[1,16]{1,0:T(1,128)} %weight_ref.1, s32[3,8]{1,0:T(4,128)} %points_ref.1, f32[8,9,2,9]{3,2,1,0:T(2,128)} %bitcast.3, f32[1,2,24,24]{3,2,1,0:T(8,128)} %shifted_ref.1, f32[2,24,24]{2,1,0:T(8,128)} %anchor_ref.1), custom_call_target="tpu_custom_call" | custom-call | tf_op jit(solution)/shard_map/pallas_call | solution.py:329
  19.2 1.4 %copy.9 = f32[1,2,9,576]{3,1,2,0:T(2,128)} copy(f32[1,2,9,576]{3,1,2,0:T(2,128)} %bitcast.2) | data formatting | bytes 82944
